TPU v7x, 32 devices: a whole 2x2x4 slice. The times are simulated.
32 devices in a mesh: dp: 8 (over z, x), mp: 4 (over y, core).
Axes of the slice: x: 2, y: 2, z: 4, core: 2. Of those that a mesh axis runs over, the one named last changes fastest.
Arguments:
- queries: bfloat16 [16, 16, 5120], P('dp', None, 'mp')
- key_value_cache: bfloat16 [128, 2, 128, 1024], P('dp', None, None, 'mp'), may hold values from -6 to 6
- slot_tags: int32 [128], P('dp'), may hold values from 0 to 15, as said below
- span_key_value: bfloat16 [16, 2, 16, 1024], P('dp', None, None, 'mp'), may hold values from -6 to 6
- answer_id: int32 [16], P('dp'), may hold values from 0 to 127
- w_cand: bfloat16 [5120, 128], P('mp')
Outputs:
- attended: bfloat16 [16, 16, 5120], P('dp', None, 'mp')
- chain_score: float32 [16], P('dp')
- answer_tally: float32 [1, 128], P(None, 'dp')
Inputs may be any that keep to these rules, and one draw needn't show every extreme that they name: `slot_tags`: among the 16 blocks of any one index of dp, at most 2 belong to the chains o * 2 to o * 2 + 1 of any one o, and for some o every index of dp holds exactly 2 such blocks. A chain may have no cached block.
All inputs are finite; a program needn't handle non-finite values.
Results may differ from a plain program's by a relative error of at most 0.0075.
Values may be sent and summed in bfloat16 or wider, within the bound.
No kernel may reach another device: no remote copies, remote signals or barrier semaphores. Data moves between devices by JAX's collectives and lax.ppermute only.
A program may use at most 128 MiB of HBM per device.

v0:
```python
import jax
import jax.numpy as jnp
from jax import lax
from jax.sharding import PartitionSpec as P

QUERY_HEADS = 40
KEY_VALUE_HEADS = 8
HEAD_SIZE = 128
NCAND = 128
PEER = 2
SAMPLES = 16


big_neg = -1e30


def block_terms(picked, blocks, causal):
    count = picked.shape[0]
    span = picked.shape[1]
    width = blocks.shape[2]
    heads_kv = blocks.shape[3] // HEAD_SIZE
    head_group = QUERY_HEADS // KEY_VALUE_HEADS
    query_rows = picked.reshape(count, span, heads_kv, head_group, HEAD_SIZE)
    lookup_matrix = blocks[:, 0].reshape(count, width, heads_kv, HEAD_SIZE)
    value_rows = blocks[:, 1].reshape(count, width, heads_kv, HEAD_SIZE)
    logit_rows = jnp.einsum(
        "nakgd,nbkd->nkgab", query_rows, lookup_matrix, preferred_element_type=jnp.float32
    ) * HEAD_SIZE ** (-0.5)
    if causal:
        allowed = jnp.arange(span)[:, None] >= jnp.arange(width)[None, :]
        logit_rows = jnp.where(allowed, logit_rows, big_neg)
    peaks = jnp.max(logit_rows, axis=-1)
    weights = jnp.exp(logit_rows - peaks[..., None])
    totals = jnp.sum(weights, axis=-1)
    summed_scores = jnp.einsum(
        "nkgab,nbkd->nkgad",
        weights.astype(jnp.bfloat16),
        value_rows,
        preferred_element_type=jnp.float32,
    )
    return (peaks, totals, summed_scores)


def merge_items(peaks, totals, summed_scores, member):
    member_f = member.astype(jnp.float32)
    masked = jnp.where(member[:, :, None, None, None], peaks[:, None], big_neg)
    chain_peak = jnp.max(masked, axis=0)
    item_peak = jnp.einsum("nc,ckga->nkga", member_f, chain_peak, precision=lax.Precision.HIGHEST)
    present = jnp.any(member, axis=1)
    factor = jnp.where(present[:, None, None, None], jnp.exp(peaks - item_peak), 0.0)
    chain_total = jnp.einsum(
        "nc,nkga->ckga", member_f, totals * factor, precision=lax.Precision.HIGHEST
    )
    chain_sum = jnp.einsum(
        "nc,nkgad->ckgad",
        member_f,
        summed_scores * factor[..., None],
        precision=lax.Precision.HIGHEST,
    )
    return (chain_peak, chain_total, chain_sum)


def fold_pair(first, second):
    overall = jnp.maximum(first[0], second[0])
    left = jnp.exp(first[0] - overall)
    right = jnp.exp(second[0] - overall)
    total = first[1] * left + second[1] * right
    summed_scores = first[2] * left[..., None] + second[2] * right[..., None]
    return (overall, total, summed_scores)


def per_device(queries, key_value_cache, slot_tags, span_key_value, answer_id, w_cand):
    accelerator_roster = lax.axis_size("dp")
    position = lax.axis_index("dp")
    chains_here = queries.shape[0]
    features = queries.shape[2]
    slots_here = slot_tags.shape[0]
    owner_index = slot_tags // chains_here
    chain_local = slot_tags % chains_here
    owner_hot = (
        owner_index[:, None] == jnp.arange(accelerator_roster, dtype=jnp.int32)[None, :]
    ).astype(jnp.int32)
    running = jnp.cumsum(owner_hot, axis=0) - 1
    rank_in = jnp.sum(owner_hot * running, axis=1)
    target = owner_index * PEER + rank_in
    places_all = accelerator_roster * PEER
    hit = (target[:, None] == jnp.arange(places_all, dtype=jnp.int32)[None, :]).astype(jnp.int32)
    source_row = jnp.sum(hit * jnp.arange(slots_here, dtype=jnp.int32)[:, None], axis=0)
    is_filled = jnp.sum(hit, axis=0) > 0
    send_chain = jnp.where(is_filled, jnp.sum(hit * chain_local[:, None], axis=0), chains_here)
    send_blocks = key_value_cache[source_row].reshape(
        (accelerator_roster, PEER) + key_value_cache.shape[1:]
    )
    send_chain = send_chain.reshape(accelerator_roster, PEER)
    blocks = lax.all_to_all(send_blocks, "dp", split_axis=0, concat_axis=0, tiled=True)
    places = lax.all_to_all(send_chain, "dp", split_axis=0, concat_axis=0, tiled=True)
    count = places.shape[0] * places.shape[1]
    flat_places = places.reshape(count)
    picked = queries[jnp.clip(flat_places, 0, chains_here - 1)]
    peaks, totals, summed_scores = block_terms(
        picked, blocks.reshape((count,) + blocks.shape[2:]), False
    )
    lead = places.shape
    peaks, totals, summed_scores, places = (
        peaks.reshape(lead + peaks.shape[1:]),
        totals.reshape(lead + totals.shape[1:]),
        summed_scores.reshape(lead + summed_scores.shape[1:]),
        places,
    )
    count = places.shape[0] * places.shape[1]
    member = places.reshape(count)[:, None] == jnp.arange(chains_here, dtype=jnp.int32)[None, :]
    remote = merge_items(
        peaks.reshape((count,) + peaks.shape[2:]),
        totals.reshape((count,) + totals.shape[2:]),
        summed_scores.reshape((count,) + summed_scores.shape[2:]),
        member,
    )
    own_span = block_terms(queries, span_key_value, True)
    final_peak, final_total, final_sum = fold_pair(own_span, remote)
    output = final_sum / final_total[..., None]
    output = jnp.transpose(output, (0, 3, 1, 2, 4)).reshape(chains_here, queries.shape[1], features)
    attended = output.astype(jnp.bfloat16)
    span = queries.shape[1]
    partial_logits = jnp.dot(
        attended.reshape(chains_here * span, features), w_cand, preferred_element_type=jnp.float32
    )
    logit_rows = lax.psum(partial_logits, "mp").reshape(chains_here, span, NCAND)
    top_logit = jnp.max(logit_rows, axis=-1, keepdims=True)
    log_norm = top_logit[..., 0] + jnp.log(jnp.sum(jnp.exp(logit_rows - top_logit), axis=-1))
    answer_hot = (answer_id[:, None] == jnp.arange(NCAND, dtype=jnp.int32)[None, :]).astype(
        jnp.float32
    )
    chosen_logit = jnp.sum(logit_rows * answer_hot[:, None, :], axis=-1)
    chain_score = jnp.mean(chosen_logit - log_norm, axis=-1)
    prompt_count = accelerator_roster * chains_here // SAMPLES
    global_chain = position * chains_here + jnp.arange(chains_here, dtype=jnp.int32)
    prompt_hot = (
        (global_chain // SAMPLES)[:, None] == jnp.arange(prompt_count, dtype=jnp.int32)[None, :]
    ).astype(jnp.float32)
    tally_terms = jnp.dot(
        prompt_hot.T, chain_score[:, None] * answer_hot, precision=lax.Precision.HIGHEST
    )
    answer_tally = lax.psum_scatter(tally_terms, "dp", scatter_dimension=1, tiled=True)
    return (attended, chain_score, answer_tally)


def solution(mesh):
    in_specs = (
        P("dp", None, "mp"),
        P("dp", None, None, "mp"),
        P("dp"),
        P("dp", None, None, "mp"),
        P("dp"),
        P("mp", None),
    )
    out_specs = (P("dp", None, "mp"), P("dp"), P(None, "dp"))
    return jax.shard_map(
        per_device, mesh=mesh, in_specs=in_specs, out_specs=out_specs, check_vma=False
    )
```

profile of v0, /device:TPU:0, one launch (start us, length us, event | category | flops | bytes accessed | tf_op | source)
XLA Modules:
  0.0 165.2 jit_solution(9929074711548436345)
XLA Ops:
  7.2 0.0 copy-start
  7.2 0.8 and_select_fusion.1
  8.0 0.1 fusion.28
  8.1 0.2 select_reduce_fusion.3
  8.3 0.1 convert_reduce_fusion
  8.4 0.7 select_n.71
  9.1 7.3 %all-to-all-start = ((s32[8,1,2]{2,1,0:T(1,128)}), s32[8,1,2]{2,1,0:T(1,128)S(1)}, u32[]{:S(2)}, u32[]{:S(2)}) async-start(s32[8,1,2]{2,1,0:T(1,128)} %bitcast.5), calls=%async_computation | async-start | bytes 8192 | tf_op jit(solution)/shard_map/all_to_all | solution.py:96
  16.4 0.0 copy-done
  16.4 2.0 %gather_fusion = bf16[16,2,128,256]{3,2,1,0:T(8,128)(2,1)} fusion(bf16[16,2,128,256]{3,2,1,0:T(8,128)(2,1)S(1)} %copy-done, s32[1024]{0:T(1024)S(1)} %pad_clamp_fusion.1), kind=kCustom, calls=%fused_computation | custom fusion | bytes 4194368 | tf_op jit(solution)/shard_map/gather | solution.py:91
  18.4 3.9 %copy.89 = bf16[8,2,2,128,256]{3,4,1,2,0:T(8,128)(2,1)} copy(bf16[8,2,2,128,256]{4,3,2,1,0:T(8,128)(2,1)} %bitcast.89) | data formatting | bytes 4194304 | tf_op jit(solution)/shard_map/reshape | solution.py:91
  22.3 0.0 copy-start.1
  22.3 0.0 copy-start.3
  22.3 0.0 copy-start.4
  22.3 0.5 all-to-all-done
  22.8 5.7 %all-to-all-start.1 = ((bf16[8,2,2,128,256]{3,4,1,2,0:T(8,128)(2,1)}), bf16[8,2,2,128,256]{3,4,1,2,0:T(8,128)(2,1)}, u32[]{:S(2)}, u32[]{:S(2)}) async-start(bf16[8,2,2,128,256]{3,4,1,2,0:T(8,128)(2,1)} %copy.89), calls=%async_computation.1 | async-start | bytes 4194304 | tf_op jit(solution)/shard_map/all_to_all | solution.py:95
  28.4 0.0 reduce-scatter.4.cloned.1.call-start
  28.5 0.0 copy-done.1
  28.5 0.1 reshape.174
  28.6 0.0 copy-done.3
  28.7 0.3 fusion.64
  29.0 0.1 fusion.18
  29.0 0.0 copy-done.4
  29.0 0.1 fusion.35
  29.1 0.5 broadcast.247
  29.6 0.7 fusion.60
  30.3 0.1 min.9
  30.4 1.4 gather_fusion.1
  31.8 1.8 %reshape.177 = bf16[16,16,2,5,128]{4,3,2,1,0:T(8,128)(2,1)S(1)} reshape(bf16[16,16,1280]{2,1,0:T(8,128)(2,1)} %gather_fusion.1) | data formatting | bytes 1310720 | tf_op jit(solution)/shard_map/reshape | solution.py:23
  33.6 0.1 eq.74
  33.7 42.5 %all-to-all-done.1 = bf16[8,2,2,128,256]{3,4,1,2,0:T(8,128)(2,1)} async-done(((bf16[8,2,2,128,256]{3,4,1,2,0:T(8,128)(2,1)}), bf16[8,2,2,128,256]{3,4,1,2,0:T(8,128)(2,1)}, u32[]{:S(2)}, u32[]{:S(2)}) %all-to-all-start.1) | async-done | bytes 2097184 | tf_op jit(solution)/shard_map/all_to_all | solution.py:95
  76.2 1.7 %copy.90 = bf16[8,2,2,128,256]{3,4,1,0,2:T(8,128)(2,1)S(1)} copy(bf16[8,2,2,128,256]{3,4,1,2,0:T(8,128)(2,1)} %all-to-all-done.1) | data formatting | bytes 4194304 | tf_op jit(solution)/shard_map/all_to_all | solution.py:95
  78.0 0.2 fusion.61
  78.2 0.6 fusion.63
  78.8 0.1 select_reduce_fusion
  78.9 0.2 fusion.12
  79.2 0.8 fusion.3
  80.0 1.4 convolution_multiply_fusion
  81.5 0.0 copy-start.2
  81.5 1.3 fusion.1
  82.8 0.2 fusion.14
  83.0 0.3 fusion.10
  83.3 0.1 convert_element_type.37
  83.4 0.0 copy-done.2
  83.4 0.2 fusion.65
  83.6 10.1 %psum.7 = f32[32,128]{1,0:T(8,128)S(1)} all-reduce(f32[32,128]{1,0:T(8,128)S(1)} %fusion.65), channel_id=1, replica_groups=mesh['dp'=8,'mp'=4] {'mp'}, use_global_device_ids=true, to_apply=%region_11.12 | all-reduce | flops 4096 | bytes 32768 | tf_op jit(solution)/shard_map/psum | solution.py:127
  93.7 0.1 reduce_max.45
  93.8 0.2 exponential_reduce_fusion
  94.0 0.1 sub.76
  94.1 0.1 reduce_sum.95
  94.2 0.0 copy-start.5
  94.3 1.0 convolution_bitcast_fusion.1
  95.2 0.0 reduce-scatter.4.cloned.1.call-update
  95.2 0.7 convert_element_type.36
  96.0 61.1 %reduce-scatter.4.cloned.1.call-done = f32[16,1]{1,0:T(8,128)} async-done(((f32[128,1]{1,0:T(8,128)}), f32[16,1]{1,0:T(8,128)}) %reduce-scatter.4.cloned.1.call-update) | async-done | bytes 80
  157.1 1.3 copy.124
  158.3 0.0 copy-done.5
  (21 shorter events, 0.3 us)
Async XLA Ops:
  7.2 9.2 %copy-start = (bf16[16,2,128,256]{3,2,1,0:T(8,128)(2,1)S(1)}, bf16[16,2,128,256]{3,2,1,0:T(8,128)(2,1)}, u32[]{:S(2)}) copy-start(bf16[16,2,128,256]{3,2,1,0:T(8,128)(2,1)} %param.7) | copy-start | bytes 6291460
  9.1 13.7 %all-to-all-start = ((s32[8,1,2]{2,1,0:T(1,128)}), s32[8,1,2]{2,1,0:T(1,128)S(1)}, u32[]{:S(2)}, u32[]{:S(2)}) async-start(s32[8,1,2]{2,1,0:T(1,128)} %bitcast.5), calls=%async_computation | async-start | bytes 8192 | tf_op jit(solution)/shard_map/all_to_all | solution.py:96
  22.3 6.2 %copy-start.1 = (bf16[2,16,1280]{2,1,0:T(8,128)(2,1)S(1)}, bf16[2,16,1280]{2,1,0:T(8,128)(2,1)}, u32[]{:S(2)}) copy-start(bf16[2,16,1280]{2,1,0:T(8,128)(2,1)} %param.6) | copy-start | bytes 245764
  22.3 6.3 %copy-start.3 = (bf16[2,2,16,256]{3,2,1,0:T(8,128)(2,1)S(1)}, bf16[2,2,16,256]{3,2,1,0:T(8,128)(2,1)}, u32[]{:S(2)}) copy-start(bf16[2,2,16,256]{3,2,1,0:T(8,128)(2,1)} %param.9) | copy-start | bytes 98308
  22.3 6.8 %copy-start.4 = (s32[2]{0:T(128)S(1)}, s32[2]{0:T(128)}, u32[]{:S(2)}) copy-start(s32[2]{0:T(128)} %param.10) | copy-start | bytes 28
  22.8 53.4 %all-to-all-start.1 = ((bf16[8,2,2,128,256]{3,4,1,2,0:T(8,128)(2,1)}), bf16[8,2,2,128,256]{3,4,1,2,0:T(8,128)(2,1)}, u32[]{:S(2)}, u32[]{:S(2)}) async-start(bf16[8,2,2,128,256]{3,4,1,2,0:T(8,128)(2,1)} %copy.89), calls=%async_computation.1 | async-start | bytes 4194304 | tf_op jit(solution)/shard_map/all_to_all | solution.py:95
  28.4 128.6 %reduce-scatter.4.cloned.1.call-start = ((), (), s32[]{:S(2)}) async-start(), calls=%async_computation.3 | async-start | bytes 73728
  81.5 1.9 %copy-start.2 = (bf16[1280,128]{1,0:T(8,128)(2,1)S(1)}, bf16[1280,128]{1,0:T(8,128)(2,1)}, u32[]{:S(2)}) copy-start(bf16[1280,128]{1,0:T(8,128)(2,1)} %param.11) | copy-start | bytes 983044
  94.2 64.1 %copy-start.5 = (f32[2]{0:T(128)}, f32[2]{0:T(128)S(1)}, u32[]{:S(2)}) copy-start(f32[2]{0:T(128)S(1)} %broadcast_multiply_fusion) | copy-start | bytes 28
Sparse Core Ops, SparseCore 0:
  95.4 61.6 reduce-scatter.3
where the time goes:
time: 166 us; the launch traced here: 165 us
  waiting for transfers between devices  104 us (63%)
  local copies, waits for them, and re-layouts  14.9 us (9%)
  between operations  14.3 us (9%)
  starting transfers between devices  13 us (8%)
  blocking collectives  10.1 us (6%)
  matrix products  5.37 us (3%)
  other arithmetic  3.42 us (2%)
    unnamed x2, waiting for transfers between devices  61.1 us
    all_to_all x1, waiting for transfers between devices, per_device(): lax.all_to_all(send_blocks, 'dp', split_axis=0, concat_axis=0, tiled=True)  42.5 us
    psum x1, blocking collectives, per_device(): lax.psum(partial_logits, 'mp').reshape(chains_here, span, NCAND)  10.1 us
    all_to_all x1, starting transfers between devices, per_device(): lax.all_to_all(send_chain, 'dp', split_axis=0, concat_axis=0, tiled=True)  7.28 us
    all_to_all x1, starting transfers between devices, per_device(): lax.all_to_all(send_blocks, 'dp', split_axis=0, concat_axis=0, tiled=True)  5.66 us
    reshape x1, local copies, waits for them, and re-layouts, per_device(): key_value_cache[source_row]  3.92 us
  transfers between devices with their start and end apart: 3, of which 3 were waited for; matrix products, arithmetic and copies ran while one was open for 7% of the time, Pallas kernels for 0%

commit v1 on v0

--- a/solution.py
+++ b/solution.py
@@ -124,7 +124,8 @@
     partial_logits = jnp.dot(
         attended.reshape(chains_here * span, features), w_cand, preferred_element_type=jnp.float32
     )
-    logit_rows = lax.psum(partial_logits, "mp").reshape(chains_here, span, NCAND)
+    gathered = lax.all_gather(partial_logits, "mp")
+    logit_rows = jnp.sum(gathered, axis=0).reshape(chains_here, span, NCAND)
     top_logit = jnp.max(logit_rows, axis=-1, keepdims=True)
     log_norm = top_logit[..., 0] + jnp.log(jnp.sum(jnp.exp(logit_rows - top_logit), axis=-1))
     answer_hot = (answer_id[:, None] == jnp.arange(NCAND, dtype=jnp.int32)[None, :]).astype(
@@ -140,7 +141,13 @@
     tally_terms = jnp.dot(
         prompt_hot.T, chain_score[:, None] * answer_hot, precision=lax.Precision.HIGHEST
     )
-    answer_tally = lax.psum_scatter(tally_terms, "dp", scatter_dimension=1, tiled=True)
+    step = 1
+    while step < accelerator_roster:
+        pairs = [(i, i ^ step) for i in range(accelerator_roster)]
+        tally_terms = tally_terms + lax.ppermute(tally_terms, "dp", pairs)
+        step *= 2
+    per = NCAND // accelerator_roster
+    answer_tally = lax.dynamic_slice_in_dim(tally_terms, position * per, per, axis=1)
     return (attended, chain_score, answer_tally)
 
 

time: 166 us -> 95.7 us (0.58)
  waiting for transfers between devices: 104 us -> 51.8 us
  between operations: 14.3 us -> 0.95 us
  blocking collectives: 10.1 us -> 5.24 us
  starting transfers between devices: 13 us -> 15 us
    unnamed x2 -> x0, waiting for transfers between devices: 61.1 us -> none
    psum x1 -> x0, blocking collectives: 10.1 us -> none  [per_device(): lax.psum(partial_logits, 'mp').reshape(chains_here, span, NCAND)]
    ppermute x0 -> x3, waiting for transfers between devices: none -> 8.77 us  [per_device(): tally_terms = tally_terms + lax.ppermute(tally_terms, 'dp', pairs)]
    all_gather x0 -> x1, blocking collectives: none -> 5.24 us  [per_device(): gathered = lax.all_gather(partial_logits, 'mp')]
    ppermute x0 -> x3, starting transfers between devices: none -> 2.11 us  [per_device(): tally_terms = tally_terms + lax.ppermute(tally_terms, 'dp', pairs)]
  transfers between devices with their start and end apart: 3 -> 5, of which waited for: 3 -> 5; matrix products, arithmetic and copies ran while one was open for 7% -> 12% of each run, Pallas kernels for 0% -> 0%
where the time goes in v1:
time: 95.7 us; the launch traced here: 95.3 us
  waiting for transfers between devices  51.8 us (54%)
  starting transfers between devices  15 us (16%)
  local copies, waits for them, and re-layouts  14.2 us (15%)
  blocking collectives  5.24 us (5%)
  matrix products  4.61 us (5%)
  other arithmetic  3.53 us (4%)
    all_to_all x1, waiting for transfers between devices, per_device(): lax.all_to_all(send_blocks, 'dp', split_axis=0, concat_axis=0, tiled=True)  42.5 us
    ppermute x3, waiting for transfers between devices, per_device(): tally_terms = tally_terms + lax.ppermute(tally_terms, 'dp', pairs)  8.77 us
    all_to_all x1, starting transfers between devices, per_device(): lax.all_to_all(send_chain, 'dp', split_axis=0, concat_axis=0, tiled=True)  7.28 us
    all_to_all x1, starting transfers between devices, per_device(): lax.all_to_all(send_blocks, 'dp', split_axis=0, concat_axis=0, tiled=True)  5.66 us
    all_gather x1, blocking collectives, per_device(): gathered = lax.all_gather(partial_logits, 'mp')  5.24 us
    reshape x1, local copies, waits for them, and re-layouts, per_device(): key_value_cache[source_row]  3.92 us
    ppermute x3, starting transfers between devices, per_device(): tally_terms = tally_terms + lax.ppermute(tally_terms, 'dp', pairs)  2.11 us
    gather x1, local copies, waits for them, and re-layouts, per_device(): key_value_cache[source_row]  1.97 us
  transfers between devices with their start and end apart: 5, of which 5 were waited for; matrix products, arithmetic and copies ran while one was open for 12% of the time, Pallas kernels for 0%

profile of v1, /device:TPU:0, one launch (start us, length us, event | category | flops | bytes accessed | tf_op | source)
XLA Modules:
  0.0 95.3 jit_solution(10765375449726532432)
XLA Ops:
  0.6 0.0 copy-start
  0.6 0.8 and_select_fusion.1
  1.5 0.1 fusion.27
  1.6 0.2 select_reduce_fusion.3
  1.8 0.1 convert_reduce_fusion
  1.9 0.7 select_n.73
  2.5 7.3 %all-to-all-start = ((s32[8,1,2]{2,1,0:T(1,128)}), s32[8,1,2]{2,1,0:T(1,128)S(1)}, u32[]{:S(2)}, u32[]{:S(2)}) async-start(s32[8,1,2]{2,1,0:T(1,128)} %bitcast.5), calls=%async_computation | async-start | bytes 8192 | tf_op jit(solution)/shard_map/all_to_all | solution.py:96
  9.8 0.0 copy-done
  9.9 2.0 %gather_fusion = bf16[16,2,128,256]{3,2,1,0:T(8,128)(2,1)} fusion(bf16[16,2,128,256]{3,2,1,0:T(8,128)(2,1)S(1)} %copy-done, s32[1024]{0:T(1024)S(1)} %pad_clamp_fusion.1), kind=kCustom, calls=%fused_computation | custom fusion | bytes 4194368 | tf_op jit(solution)/shard_map/gather | solution.py:91
  11.8 3.9 %copy.89 = bf16[8,2,2,128,256]{3,4,1,2,0:T(8,128)(2,1)} copy(bf16[8,2,2,128,256]{4,3,2,1,0:T(8,128)(2,1)} %bitcast.84) | data formatting | bytes 4194304 | tf_op jit(solution)/shard_map/reshape | solution.py:91
  15.8 0.0 copy-start.1
  15.8 0.0 copy-start.3
  15.8 0.0 copy-start.4
  15.8 0.5 all-to-all-done
  16.2 5.7 %all-to-all-start.1 = ((bf16[8,2,2,128,256]{3,4,1,2,0:T(8,128)(2,1)}), bf16[8,2,2,128,256]{3,4,1,2,0:T(8,128)(2,1)}, u32[]{:S(2)}, u32[]{:S(2)}) async-start(bf16[8,2,2,128,256]{3,4,1,2,0:T(8,128)(2,1)} %copy.89), calls=%async_computation.1 | async-start | bytes 4194304 | tf_op jit(solution)/shard_map/all_to_all | solution.py:95
  21.9 0.0 copy-done.1
  21.9 0.1 reshape.181
  22.0 0.0 copy-done.3
  22.1 0.3 fusion.61
  22.4 0.1 fusion.18
  22.5 0.0 copy-done.4
  22.5 0.1 fusion.33
  22.5 0.5 broadcast.239
  23.0 0.7 fusion.57
  23.7 0.1 min.9
  23.8 1.4 %gather_fusion.1 = bf16[16,16,1280]{2,1,0:T(8,128)(2,1)} fusion(bf16[2,16,1280]{2,1,0:T(8,128)(2,1)S(1)} %copy-done.1, s32[1024]{0:T(1024)S(1)} %pad_clamp_fusion), kind=kCustom, calls=%fused_computation.1 | custom fusion | bytes 1310784 | tf_op jit(solution)/shard_map/gather | solution.py:99
  25.3 1.8 %reshape.184 = bf16[16,16,2,5,128]{4,3,2,1,0:T(8,128)(2,1)S(1)} reshape(bf16[16,16,1280]{2,1,0:T(8,128)(2,1)} %gather_fusion.1) | data formatting | bytes 1310720 | tf_op jit(solution)/shard_map/reshape | solution.py:23
  27.1 0.1 eq.73
  27.2 42.5 %all-to-all-done.1 = bf16[8,2,2,128,256]{3,4,1,2,0:T(8,128)(2,1)} async-done(((bf16[8,2,2,128,256]{3,4,1,2,0:T(8,128)(2,1)}), bf16[8,2,2,128,256]{3,4,1,2,0:T(8,128)(2,1)}, u32[]{:S(2)}, u32[]{:S(2)}) %all-to-all-start.1) | async-done | bytes 2097184 | tf_op jit(solution)/shard_map/all_to_all | solution.py:95
  69.7 1.7 %copy.90 = bf16[8,2,2,128,256]{3,4,1,0,2:T(8,128)(2,1)S(1)} copy(bf16[8,2,2,128,256]{3,4,1,2,0:T(8,128)(2,1)} %all-to-all-done.1) | data formatting | bytes 4194304 | tf_op jit(solution)/shard_map/all_to_all | solution.py:95
  71.4 0.2 fusion.58
  71.6 0.6 fusion.60
  72.2 0.1 select_reduce_fusion
  72.4 0.2 fusion.12
  72.7 0.8 fusion.3
  73.5 1.4 %convolution_multiply_fusion = f32[16,2,5,16,128]{4,3,2,1,0:T(8,128)S(1)} fusion(bf16[16,128,2,128,1]{1,3,4,2,0:T(8,128)(2,1)S(1)} %bitcast.86, f32[16,2,5,16,128]{4,3,2,1,0:T(8,128)S(1)} %get-tuple-element.19, f32[16,2,5,16]{3,2,1,0:T(8,128)S(1)} %copy.99, f32[16,2,5,16]{3,2,1,0:T(8,128)S(1)} %get-tuple-element.18), kind=kOutput, calls=%fused_computation.2 | convolution fusion | flops 84869120 | bytes 3690496 | tf_op jit(solution)/shard_map/nkgab,nbkd->nkgad/dot_general | solution.py:35
  74.9 0.0 copy-start.2
  74.9 1.3 %fusion.1 = f32[2,2,5,16,128]{4,0,3,2,1:T(2,128)S(1)} fusion(f32[16,2,5,16,128]{4,3,2,1,0:T(8,128)S(1)} %convolution_multiply_fusion, s32[16]{0:T(128)S(1)} %eq.73), kind=kOutput, calls=%fused_computation.5 | convolution fusion | flops 7864352 | bytes 1474624 | tf_op jit(solution)/shard_map/nc,nkgad->ckgad/dot_general | solution.py:54
  76.3 0.2 fusion.14
  76.4 0.3 fusion.10
  76.8 0.1 convert_element_type.37
  76.9 0.0 copy-done.2
  76.9 0.2 fusion.62
  77.1 5.2 %all-gather = f32[128,128]{1,0:T(8,128)S(1)} all-gather(f32[32,128]{1,0:T(8,128)S(1)} %fusion.62), channel_id=2, replica_groups=mesh['dp'=8,'mp'=4] {'mp'}, dimensions={0}, use_global_device_ids=true | all-gather | bytes 81920 | tf_op jit(solution)/shard_map/all_gather | solution.py:127
  82.3 0.1 reduce_max.45
  82.4 0.2 exponential_reduce_fusion
  82.6 0.1 add.75
  82.7 0.1 multiply_reduce_fusion
  82.8 0.1 subtract_reduce_fusion
  82.9 0.0 copy-start.5
  82.9 0.2 fusion.31
  83.1 1.5 %collective-permute-start = (f32[1,128]{1,0:T(1,128)S(1)}, f32[1,128]{1,0:T(1,128)S(1)}, u32[]{:S(2)}, u32[]{:S(2)}) collective-permute-start(f32[1,128]{1,0:T(1,128)S(1)} %fusion.31), channel_id=1, source_target_pairs={{0,4},{4,0},{8,12},{12,8},{16,20},{20,16},{24,28},{28,24},{1,5},{5... | collective-permute-start | bytes 1544 | tf_op jit(solution)/shard_map/ppermute | solution.py:147
  84.6 2.1 %collective-permute-done = f32[1,128]{1,0:T(1,128)S(1)} collective-permute-done((f32[1,128]{1,0:T(1,128)S(1)}, f32[1,128]{1,0:T(1,128)S(1)}, u32[]{:S(2)}, u32[]{:S(2)}) %collective-permute-start) | collective-permute-done | bytes 544 | tf_op jit(solution)/shard_map/ppermute | solution.py:147
  86.7 0.0 collective-permute-start.1
  86.7 3.6 %collective-permute-done.1 = f32[1,128]{1,0:T(1,128)S(1)} collective-permute-done((f32[1,128]{1,0:T(1,128)S(1)}, f32[1,128]{1,0:T(1,128)S(1)}, u32[]{:S(2)}, u32[]{:S(2)}) %collective-permute-start.1) | collective-permute-done | bytes 544 | tf_op jit(solution)/shard_map/ppermute | solution.py:147
  90.3 0.6 collective-permute-start.2
  90.9 0.7 convert_element_type.36
  91.7 3.1 %collective-permute-done.2 = f32[1,128]{1,0:T(1,128)S(1)} collective-permute-done((f32[1,128]{1,0:T(1,128)S(1)}, f32[1,128]{1,0:T(1,128)S(1)}, u32[]{:S(2)}, u32[]{:S(2)}) %collective-permute-start.2) | collective-permute-done | bytes 544 | tf_op jit(solution)/shard_map/ppermute | solution.py:147
  94.8 0.6 constant_dynamic-slice_fusion
  95.3 0.0 copy-done.5
  (25 shorter events, 0.3 us)
Async XLA Ops:
  0.6 9.2 %copy-start = (bf16[16,2,128,256]{3,2,1,0:T(8,128)(2,1)S(1)}, bf16[16,2,128,256]{3,2,1,0:T(8,128)(2,1)}, u32[]{:S(2)}) copy-start(bf16[16,2,128,256]{3,2,1,0:T(8,128)(2,1)} %param.7) | copy-start | bytes 6291460
  2.5 13.7 %all-to-all-start = ((s32[8,1,2]{2,1,0:T(1,128)}), s32[8,1,2]{2,1,0:T(1,128)S(1)}, u32[]{:S(2)}, u32[]{:S(2)}) async-start(s32[8,1,2]{2,1,0:T(1,128)} %bitcast.5), calls=%async_computation | async-start | bytes 8192 | tf_op jit(solution)/shard_map/all_to_all | solution.py:96
  15.8 6.1 %copy-start.1 = (bf16[2,16,1280]{2,1,0:T(8,128)(2,1)S(1)}, bf16[2,16,1280]{2,1,0:T(8,128)(2,1)}, u32[]{:S(2)}) copy-start(bf16[2,16,1280]{2,1,0:T(8,128)(2,1)} %param.6) | copy-start | bytes 245764
  15.8 6.3 %copy-start.3 = (bf16[2,2,16,256]{3,2,1,0:T(8,128)(2,1)S(1)}, bf16[2,2,16,256]{3,2,1,0:T(8,128)(2,1)}, u32[]{:S(2)}) copy-start(bf16[2,2,16,256]{3,2,1,0:T(8,128)(2,1)} %param.9) | copy-start | bytes 98308
  15.8 6.7 %copy-start.4 = (s32[2]{0:T(128)S(1)}, s32[2]{0:T(128)}, u32[]{:S(2)}) copy-start(s32[2]{0:T(128)} %param.10) | copy-start | bytes 28
  16.2 53.4 %all-to-all-start.1 = ((bf16[8,2,2,128,256]{3,4,1,2,0:T(8,128)(2,1)}), bf16[8,2,2,128,256]{3,4,1,2,0:T(8,128)(2,1)}, u32[]{:S(2)}, u32[]{:S(2)}) async-start(bf16[8,2,2,128,256]{3,4,1,2,0:T(8,128)(2,1)} %copy.89), calls=%async_computation.1 | async-start | bytes 4194304 | tf_op jit(solution)/shard_map/all_to_all | solution.py:95
  74.9 1.9 %copy-start.2 = (bf16[1280,128]{1,0:T(8,128)(2,1)S(1)}, bf16[1280,128]{1,0:T(8,128)(2,1)}, u32[]{:S(2)}) copy-start(bf16[1280,128]{1,0:T(8,128)(2,1)} %param.11) | copy-start | bytes 983044
  82.9 12.4 %copy-start.5 = (f32[2]{0:T(128)}, f32[2]{0:T(128)S(1)}, u32[]{:S(2)}) copy-start(f32[2]{0:T(128)S(1)} %broadcast_multiply_fusion) | copy-start | bytes 28
  83.1 3.6 %collective-permute-start = (f32[1,128]{1,0:T(1,128)S(1)}, f32[1,128]{1,0:T(1,128)S(1)}, u32[]{:S(2)}, u32[]{:S(2)}) collective-permute-start(f32[1,128]{1,0:T(1,128)S(1)} %fusion.31), channel_id=1, source_target_pairs={{0,4},{4,0},{8,12},{12,8},{16,20},{20,16},{24,28},{28,24},{1,5},{5... | collective-permute-start | bytes 1544 | tf_op jit(solution)/shard_map/ppermute | solution.py:147
  86.7 3.6 %collective-permute-start.1 = (f32[1,128]{1,0:T(1,128)S(1)}, f32[1,128]{1,0:T(1,128)S(1)}, u32[]{:S(2)}, u32[]{:S(2)}) collective-permute-start(f32[1,128]{1,0:T(1,128)S(1)} %add.78), channel_id=1, source_target_pairs={{0,8},{4,12},{8,0},{12,4},{16,24},{20,28},{24,16},{28,20},{1,9},{5... | collective-permute-start | bytes 1544 | tf_op jit(solution)/shard_map/ppermute | solution.py:147
  90.3 4.5 %collective-permute-start.2 = (f32[1,128]{1,0:T(1,128)S(1)}, f32[1,128]{1,0:T(1,128)S(1)}, u32[]{:S(2)}, u32[]{:S(2)}) collective-permute-start(f32[1,128]{1,0:T(1,128)S(1)} %add.79), channel_id=1, source_target_pairs={{0,16},{4,20},{8,24},{12,28},{16,0},{20,4},{24,8},{28,12},{1,17},{... | collective-permute-start | bytes 1544 | tf_op jit(solution)/shard_map/ppermute | solution.py:147
